TPU v7x, 128 devices: a whole 4x4x4 slice. The times are simulated.
128 devices in a mesh: dp: 8 (over x, core), mp: 16 (over z, y).
Axes of the slice: x: 4, y: 4, z: 4, core: 2. Of those that a mesh axis runs over, the one named last changes fastest.
Arguments:
- tokens: bfloat16 [2048, 8192], P('dp'), may hold values from -6 to 6
- norm_gain: float32 [8192], replicated, may hold values from 0.5 to 1.5
- gate_weight: bfloat16 [8192, 28672], P('dp', 'mp'), may hold values from -0.0625 to 0.0625
- gate_mask: int32 [8192, 896], P('dp', 'mp'), may hold values from -2147483648 to 2147483646
- up_weight: bfloat16 [8192, 28672], P('dp', 'mp'), may hold values from -0.0625 to 0.0625
- up_mask: int32 [8192, 896], P('dp', 'mp'), may hold values from -2147483648 to 2147483646
- down_weight: bfloat16 [28672, 8192], P('mp', 'dp'), may hold values from -0.03125 to 0.03125
- down_mask: int32 [28672, 256], P('mp', 'dp'), may hold values from -2147483648 to 2147483647, as said below
Outputs:
- mixed: bfloat16 [2048, 8192], P('mp', 'dp')
- input_norms: float32 [8192], P('dp')
- hidden_norms: float32 [28672], P('mp')
Inputs may be any that keep to these rules, and one draw needn't show every extreme that they name: `down_mask`: in every word each of the eight aligned groups of four bits holds exactly two ones, so exactly two of every four consecutive columns of the down projection are kept.
All inputs are finite; a program needn't handle non-finite values.
Results may differ from a plain program's by a relative error of at most 0.025.
Values may be sent and summed in bfloat16 or wider, within the bound.
No kernel may reach another device: no remote copies, remote signals or barrier semaphores. Data moves between devices by JAX's collectives and lax.ppermute only.
A program may use at most 128 MiB of HBM per device.

v0:
```python
import jax
import jax.numpy as jnp
from jax import lax
from jax.sharding import Mesh
from jax.sharding import PartitionSpec as P

MP = ("mp_0", "mp_1")


def sent_to_all(array, axis):
    length = lax.axis_size(axis)
    return lax.all_to_all(
        jnp.broadcast_to(array[None], (length, *array.shape)), axis, 0, 0, tiled=True
    )


def over_copies(array, axis):
    return sent_to_all(array, axis).sum(axis=0)


def sum_by_axis(array, axes, dim):
    for axis in axes:
        array = lax.psum_scatter(array, axis, scatter_dimension=dim, tiled=True)
    return array


def keep_entries(weight, packed):
    shifts = jnp.arange(32, dtype=jnp.int32)
    kept_bits = jnp.right_shift(packed[..., None], shifts) & 1
    kept_bits = kept_bits.reshape(weight.shape)
    return jnp.where(kept_bits == 1, weight, jnp.zeros_like(weight))


def on_device(
    tokens, norm_gain, gate_weight, gate_mask, up_weight, up_mask, down_weight, down_mask
):
    values = tokens.astype(jnp.float32)
    scale = lax.rsqrt(jnp.mean(values * values, axis=1, keepdims=True) + 1e-05)
    normed = (values * scale * norm_gain).astype(jnp.bfloat16)
    columns = lax.all_to_all(normed, "dp", split_axis=1, concat_axis=0, tiled=True)
    widened = columns.astype(jnp.float32)
    input_norms = jnp.sqrt(jnp.sum(widened * widened, axis=0))
    gate_kept = keep_entries(gate_weight, gate_mask)
    up_kept = keep_entries(up_weight, up_mask)
    down_kept = keep_entries(down_weight, down_mask)
    units = gate_kept.shape[1]
    gate_part = jnp.dot(columns, gate_kept, preferred_element_type=jnp.float32)
    up_part = jnp.dot(columns, up_kept, preferred_element_type=jnp.float32)
    both_sums = lax.psum_scatter(
        jnp.concatenate([gate_part, up_part], axis=1).astype(jnp.bfloat16),
        "dp",
        scatter_dimension=0,
        tiled=True,
    ).astype(jnp.float32)
    hidden = (jax.nn.silu(both_sums[:, :units]) * both_sums[:, units:]).astype(jnp.bfloat16)
    wide_hidden = hidden.astype(jnp.float32)
    squares = over_copies(jnp.sum(wide_hidden * wide_hidden, axis=0), "dp")
    hidden_norms = jnp.sqrt(squares)
    partial_out = jnp.dot(
        lax.all_gather(hidden, "dp", axis=0, tiled=True),
        down_kept,
        preferred_element_type=jnp.float32,
    )
    mixed = (
        sum_by_axis(partial_out.astype(jnp.bfloat16), MP, 0)
        .astype(jnp.float32)
        .astype(jnp.bfloat16)
    )
    return (mixed, input_norms, hidden_norms)


def solution(mesh):
    finer = Mesh(mesh.devices.reshape(mesh.shape["dp"], 4, 4), ("dp", "mp_0", "mp_1"))
    in_specs = (
        P("dp", None),
        P(),
        P("dp", MP),
        P("dp", MP),
        P("dp", MP),
        P("dp", MP),
        P(MP, "dp"),
        P(MP, "dp"),
    )
    out_specs = (P(MP, "dp"), P("dp"), P(MP))
    return jax.shard_map(
        on_device, mesh=finer, in_specs=in_specs, out_specs=out_specs, check_vma=False
    )
```

profile of v0, /device:TPU:0, one launch (start us, length us, event | category | flops | bytes accessed | tf_op | source)
XLA Modules:
  0.0 346.1 jit_solution(16962766649375081931)
XLA Ops:
  7.2 6.4 %copy.27 = bf16[256,8192]{0,1:T(8,128)(2,1)} copy(bf16[256,8192]{1,0:T(8,128)(2,1)} %param.8) | data formatting | bytes 8388608 | tf_op args[0]
  13.5 3.5 fusion
  17.0 2.6 fusion.2
  19.7 4.6 %all-to-all-start = ((bf16[256,8,1024]{0,2,1:T(8,128)(2,1)}), bf16[256,8,1024]{0,2,1:T(8,128)(2,1)}, u32[]{:S(2)}, u32[]{:S(2)}) async-start(bf16[256,8,1024]{0,2,1:T(8,128)(2,1)} %bitcast.34), calls=%async_computation | async-start | bytes 8388608 | tf_op jit(solution)/shard_map/all_to_all | solution.py:40
  24.2 0.2 reduce-scatter.4.cloned.1.call-start
  24.5 0.1 shift_right_arithmetic.63
  24.5 6.0 %copy.29 = bf16[1024,1792]{0,1:T(8,128)(2,1)} copy(bf16[1024,1792]{1,0:T(8,128)(2,1)} %param.10) | data formatting | bytes 7340032 | tf_op args[2]
  30.5 6.0 %copy.30 = bf16[1024,1792]{0,1:T(8,128)(2,1)} copy(bf16[1024,1792]{1,0:T(8,128)(2,1)} %param.12) | data formatting | bytes 7340032 | tf_op args[4]
  36.5 6.7 %fusion.9 = (bf16[1024,1792]{0,1:T(8,128)(2,1)}, bf16[1024,1792]{0,1:T(8,128)(2,1)}) fusion(bf16[1024,1792]{0,1:T(8,128)(2,1)} %copy.29, s32[1792]{0:T(1024)S(1)} %shift_right_arithmetic.63, s32[1024,56]{0,1:T(8,128)S(1)} %copy-done.3, bf16[1024,1792]{0,1:T(8,128)(2,1)} %copy.30, s32[1024,56]{0,1:T(8,128)S(1)} %copy-done.4), kind=kLoop, calls=%fused_computation.18 | loop fusion | flops 14680064 | bytes 15145984 | tf_op jit(solution)/shard_map/jit(_where)/select_n | solution.py:31
  43.2 30.6 %all-to-all-done = bf16[256,8,1024]{0,2,1:T(8,128)(2,1)} async-done(((bf16[256,8,1024]{0,2,1:T(8,128)(2,1)}), bf16[256,8,1024]{0,2,1:T(8,128)(2,1)}, u32[]{:S(2)}, u32[]{:S(2)}) %all-to-all-start) | async-done | bytes 4194336 | tf_op jit(solution)/shard_map/all_to_all | solution.py:40
  73.9 6.5 %copy.28 = bf16[8,256,1024]{2,1,0:T(8,128)(2,1)} copy(bf16[8,256,1024]{1,2,0:T(8,128)(2,1)} %bitcast.1) | data formatting | bytes 8388608 | tf_op jit(solution)/shard_map/all_to_all | solution.py:40
  80.3 10.9 %convolution_convert_fusion = bf16[2048,1792]{0,1:T(8,128)(2,1)S(1)} fusion(bf16[2048,1024]{1,0:T(8,128)(2,1)} %bitcast.35, bf16[1024,1792]{0,1:T(8,128)(2,1)} %get-tuple-element.6), kind=kOutput, calls=%fused_computation.7 | convolution fusion | flops 7519862784 | bytes 15204352 | tf_op jit(solution)/shard_map/dot_general | solution.py:48
  91.3 8.4 %convolution_convert_fusion.1 = bf16[2048,1792]{0,1:T(8,128)(2,1)S(1)} fusion(bf16[2048,1024]{1,0:T(8,128)(2,1)S(1)} %bitcast.36, bf16[1024,1792]{0,1:T(8,128)(2,1)S(1)} %copy-done.2), kind=kOutput, calls=%fused_computation.8 | convolution fusion | flops 7519862784 | bytes 15204352 | tf_op jit(solution)/shard_map/dot_general | solution.py:47
  99.7 17.1 %pad_maximum_fusion = bf16[2048,3584]{0,1:T(8,128)(2,1)} fusion(bf16[2048,1792]{0,1:T(8,128)(2,1)S(1)} %convolution_convert_fusion, bf16[2048,1792]{0,1:T(8,128)(2,1)S(1)} %convolution_convert_fusion.1), kind=kLoop, calls=%fused_computation | loop fusion | flops 29360128 | bytes 29360128 | tf_op jit(solution)/shard_map/concatenate | solution.py:50
  116.8 0.0 all-gather.2.cloned.1.call-start
  116.9 83.1 %reduce-scatter.4.cloned.1.call-done = bf16[256,3584]{0,1:T(8,128)(2,1)} async-done(((bf16[2048,3584]{0,1:T(8,128)(2,1)}), bf16[256,3584]{0,1:T(8,128)(2,1)}) %reduce-scatter.4.cloned.1.call-update) | async-done | bytes 1835024 | tf_op jit(solution)/shard_map/reduce_scatter | solution.py:49
  199.9 1.8 convert_element_type.27
  201.7 1.5 multiply_reduce_fusion.1
  203.3 0.3 reduce-scatter.6.cloned.1.call-start
  203.5 0.1 shift_right_arithmetic.72
  203.6 5.9 %copy.31 = bf16[1792,1024]{0,1:T(8,128)(2,1)} copy(bf16[1792,1024]{1,0:T(8,128)(2,1)} %param.14) | data formatting | bytes 7340032 | tf_op args[6]
  209.5 4.5 %fusion.11 = bf16[1792,1024]{0,1:T(8,128)(2,1)} fusion(bf16[1792,1024]{0,1:T(8,128)(2,1)} %copy.31, s32[1024]{0:T(1024)S(1)} %shift_right_arithmetic.72, s32[1792,32]{0,1:T(8,128)S(1)} %copy-done.5), kind=kLoop, calls=%fused_computation.20 | loop fusion | flops 7340032 | bytes 7573504 | tf_op jit(solution)/shard_map/jit(_where)/select_n | solution.py:31
  214.0 37.9 %all-gather.2.cloned.1.call-done = bf16[2048,1792]{0,1:T(8,128)(2,1)} async-done(((bf16[256,1792]{0,1:T(8,128)(2,1)}), bf16[2048,1792]{0,1:T(8,128)(2,1)}) %all-gather.2.cloned.1.call-update) | async-done | bytes 7340048 | tf_op jit(solution)/shard_map/all_gather | solution.py:60
  251.9 13.2 %convolution_convert_fusion.2 = bf16[2048,1024]{1,0:T(8,128)(2,1)} fusion(bf16[2048,1792]{0,1:T(8,128)(2,1)} %all-gather.2.cloned.1.call-done, bf16[1792,1024]{0,1:T(8,128)(2,1)} %fusion.11), kind=kOutput, calls=%fused_computation.21 | convolution fusion | flops 7518289920 | bytes 15204352 | tf_op jit(solution)/shard_map/dot_general | solution.py:59
  265.2 48.1 %reduce-scatter.6.cloned.1.call-done = bf16[512,1024]{1,0:T(8,128)(2,1)} async-done(((bf16[2048,1024]{1,0:T(8,128)(2,1)}), bf16[512,1024]{1,0:T(8,128)(2,1)}) %reduce-scatter.6.cloned.1.call-update) | async-done | bytes 1048592 | tf_op jit(solution)/shard_map/reduce_scatter | solution.py:23
  313.4 0.6 broadcast_in_dim.5
  314.0 4.3 %all-to-all-start.1 = ((f32[8,1,1792]{2,1,0:T(1,128)}), f32[8,1,1792]{2,1,0:T(1,128)S(1)}, u32[]{:S(2)}, u32[]{:S(2)}) async-start(f32[8,1,1792]{2,1,0:T(1,128)} %broadcast_in_dim.5), calls=%async_computation.4 | async-start | bytes 114688 | tf_op jit(solution)/shard_map/all_to_all | solution.py:12
  318.3 3.1 multiply_reduce_fusion
  321.3 0.6 sqrt.6
  321.9 1.9 all-to-all-done.1
  323.9 0.6 sqrt.7
  324.5 15.1 %reduce-scatter.8.cloned.1.call-done = bf16[128,1024]{1,0:T(8,128)(2,1)} async-done(((bf16[512,1024]{1,0:T(8,128)(2,1)}), bf16[128,1024]{1,0:T(8,128)(2,1)}) %reduce-scatter.8.cloned.1.call-update) | async-done | bytes 262160 | tf_op jit(solution)/shard_map/reduce_scatter | solution.py:23
  (23 shorter events, 0.2 us)
Async XLA Ops:
  7.2 9.8 %copy-start.6 = (f32[8192]{0:T(1024)S(1)}, f32[8192]{0:T(1024)}, u32[]{:S(2)}) copy-start(f32[8192]{0:T(1024)} %param.9) | copy-start | bytes 98308
  13.5 3.5 %copy-start = (bf16[256,8192]{0,1:T(8,128)(2,1)S(1)}, bf16[256,8192]{0,1:T(8,128)(2,1)}, u32[]{:S(2)}) copy-start(bf16[256,8192]{0,1:T(8,128)(2,1)} %copy.27) | copy-start | bytes 12582916
  19.7 54.2 %all-to-all-start = ((bf16[256,8,1024]{0,2,1:T(8,128)(2,1)}), bf16[256,8,1024]{0,2,1:T(8,128)(2,1)}, u32[]{:S(2)}, u32[]{:S(2)}) async-start(bf16[256,8,1024]{0,2,1:T(8,128)(2,1)} %bitcast.34), calls=%async_computation | async-start | bytes 8388608 | tf_op jit(solution)/shard_map/all_to_all | solution.py:40
  24.2 175.7 %reduce-scatter.4.cloned.1.call-start = ((), (), s32[]{:S(2)}) async-start(), calls=%async_computation.5 | async-start | bytes 16515072 | tf_op jit(solution)/shard_map/reduce_scatter | solution.py:49
  30.5 6.0 %copy-start.3 = (s32[1024,56]{0,1:T(8,128)S(1)}, s32[1024,56]{0,1:T(8,128)}, u32[]{:S(2)}) copy-start(s32[1024,56]{0,1:T(8,128)} %param.11) | copy-start | bytes 688132
  30.5 6.0 %copy-start.4 = (s32[1024,56]{0,1:T(8,128)S(1)}, s32[1024,56]{0,1:T(8,128)}, u32[]{:S(2)}) copy-start(s32[1024,56]{0,1:T(8,128)} %param.13) | copy-start | bytes 688132
  80.3 10.9 %copy-start.1 = (bf16[8,256,1024]{2,1,0:T(8,128)(2,1)S(1)}, bf16[8,256,1024]{2,1,0:T(8,128)(2,1)}, u32[]{:S(2)}) copy-start(bf16[8,256,1024]{2,1,0:T(8,128)(2,1)} %copy.28) | copy-start | bytes 12582916
  80.3 10.9 %copy-start.2 = (bf16[1024,1792]{0,1:T(8,128)(2,1)S(1)}, bf16[1024,1792]{0,1:T(8,128)(2,1)}, u32[]{:S(2)}) copy-start(bf16[1024,1792]{0,1:T(8,128)(2,1)} %get-tuple-element.5) | copy-start | bytes 11010052
  116.8 135.1 %all-gather.2.cloned.1.call-start = ((), (), s32[]{:S(2)}) async-start(), calls=%async_computation.6 | async-start | bytes 8257536 | tf_op jit(solution)/shard_map/all_gather | solution.py:60
  203.2 6.3 %copy-start.5 = (s32[1792,32]{0,1:T(8,128)S(1)}, s32[1792,32]{0,1:T(8,128)}, u32[]{:S(2)}) copy-start(s32[1792,32]{0,1:T(8,128)} %param.15) | copy-start | bytes 688132
  203.3 110.1 %reduce-scatter.6.cloned.1.call-start = ((), (), s32[]{:S(2)}) async-start(), calls=%async_computation.7 | async-start | bytes 5242880 | tf_op jit(solution)/shard_map/reduce_scatter | solution.py:23
  265.2 74.4 %reduce-scatter.8.cloned.1.call-start = ((), (), s32[]{:S(2)}) async-start(), calls=%async_computation.8 | async-start | bytes 1310720 | tf_op jit(solution)/shard_map/reduce_scatter | solution.py:23
  314.0 9.8 %all-to-all-start.1 = ((f32[8,1,1792]{2,1,0:T(1,128)}), f32[8,1,1792]{2,1,0:T(1,128)S(1)}, u32[]{:S(2)}, u32[]{:S(2)}) async-start(f32[8,1,1792]{2,1,0:T(1,128)} %broadcast_in_dim.5), calls=%async_computation.4 | async-start | bytes 114688 | tf_op jit(solution)/shard_map/all_to_all | solution.py:12
Sparse Core Ops, SparseCore 0:
  116.9 82.9 reduce-scatter.3
  203.4 48.4 all-gather.1
  265.3 48.0 reduce-scatter.5
  316.2 23.3 reduce-scatter.7
where the time goes:
time: 347 us; the launch traced here: 346 us
  waiting for transfers between devices  217 us (63%)
  other arithmetic  40.8 us (12%)
  local copies, waits for them, and re-layouts  32.7 us (9%)
  matrix products  32.5 us (9%)
  between operations  13.9 us (4%)
  starting transfers between devices  9.37 us (3%)
    reduce_scatter x1, waiting for transfers between devices, on_device(): lax.psum_scatter(jnp.concatenate([gate_part, up_part], axis=1).astype(jnp...  83.1 us
    reduce_scatter x2, waiting for transfers between devices, sum_by_axis(): array = lax.psum_scatter(array, axis, scatter_dimension=dim, tiled=True)  63.2 us
    all_gather x1, waiting for transfers between devices, on_device(): lax.all_gather(hidden, 'dp', axis=0, tiled=True)  37.9 us
    all_to_all x1, waiting for transfers between devices, on_device(): lax.all_to_all(normed, 'dp', split_axis=1, concat_axis=0, tiled=True)  30.6 us
    unnamed x18, local copies, waits for them, and re-layouts  24.2 us
    concatenate x1, other arithmetic, on_device(): jnp.concatenate([gate_part, up_part], axis=1).astype(jnp.bfloat16)  17.1 us
    dot_general x1, matrix products, on_device(): jnp.dot(lax.all_gather(hidden, 'dp', axis=0, tiled=True), down_kept, pref...  13.2 us
    select_n x2, other arithmetic, keep_entries(): return jnp.where(kept_bits == 1, weight, jnp.zeros_like(weight))  11.2 us
  transfers between devices with their start and end apart: 6, of which 6 were waited for; matrix products, arithmetic and copies ran while one was open for 10% of the time, Pallas kernels for 0%

commit v1 on v0

v1 whole, which is shorter than its diff:
```python
import jax
import jax.numpy as jnp
from jax import lax
from jax.experimental import pallas as pl
from jax.experimental.pallas import tpu as pltpu
from jax.sharding import Mesh
from jax.sharding import PartitionSpec as P

DP = ("x", "c")
MP = ("z", "y")
BF = jnp.bfloat16
F32 = jnp.float32
SPLIT = (64, 64)
FULL_TILE = 1792
SMALL_TILE = 256
DOWN_TILE = 512
MASK_ROWS = 128

VMEM = pl.BlockSpec(memory_space=pltpu.VMEM)
SMEM = pl.BlockSpec(memory_space=pltpu.SMEM)
HBM = pl.BlockSpec(memory_space=pltpu.HBM)


def params(mib=24):
    return pltpu.CompilerParams(vmem_limit_bytes=mib * 1024 * 1024)


def in_hbm(array):
    return pltpu.with_memory_space_constraint(array, pltpu.HBM)


def in_vmem(array):
    return pltpu.with_memory_space_constraint(array, pltpu.VMEM)


def cost(flops, nbytes):
    return pl.CostEstimate(flops=int(flops), bytes_accessed=int(nbytes), transcendentals=0)


def shift(array, axis, by):
    size = lax.axis_size(axis)
    return lax.ppermute(array, axis, [(i, (i + by) % size) for i in range(size)])


def swap(array):
    return lax.ppermute(array, "c", [(0, 1), (1, 0)])


def norm_call(idx, tokens, gain, dists, which=None):
    rows, width = tokens.shape
    nx = 4
    part = width // nx
    block = rows // 4
    steps = 4 if which is None else 1

    def body(idx_ref, tok_hbm, gain_hbm, *rest):
        out_refs = rest[: len(dists)]
        tok_ref, gain_ref, sems = rest[len(dists) :]
        copies = [pltpu.make_async_copy(gain_hbm, gain_ref, sems.at[steps])]
        for i in range(steps):
            at = i * block if which is None else pl.multiple_of(idx_ref[which] * block, block)
            src = tok_hbm.at[pl.ds(at, block), :]
            copies.append(pltpu.make_async_copy(src, tok_ref.at[i], sems.at[i]))
        for copy in copies:
            copy.start()
        copies[0].wait()
        for i in range(steps):
            copies[1 + i].wait()
            v = tok_ref[i].astype(F32)
            scale = lax.rsqrt(jnp.mean(v * v, axis=1, keepdims=True) + 1e-05)
            for d, out_ref in zip(dists, out_refs):
                cut = pl.ds(pl.multiple_of(lax.rem(idx_ref[0] + d, nx) * part, part), part)
                v = tok_ref[i, :, cut].astype(F32)
                out_ref[i * block : (i + 1) * block] = (v * scale * gain_ref[:, cut]).astype(BF)

    return pl.pallas_call(
        body,
        out_shape=[jax.ShapeDtypeStruct((steps * block, part), BF)] * len(dists),
        in_specs=[SMEM, HBM, HBM],
        out_specs=[VMEM] * len(dists),
        scratch_shapes=[
            pltpu.VMEM((steps, block, width), BF),
            pltpu.VMEM((1, width), F32),
            pltpu.SemaphoreType.DMA((steps + 1,)),
        ],
        compiler_params=params(10),
        cost_estimate=cost(5e8 * steps, 2e6 * steps),
        name="norm",
    )(idx, in_hbm(tokens), in_hbm(gain.reshape(1, width)))


def spread(mask_t, columns):
    parts = [jnp.bitwise_and(jnp.right_shift(mask_t, 8 * b), 255) for b in range(4)]
    stacked = jnp.concatenate([p.astype(F32) for p in parts], axis=0).astype(BF)
    return lax.dot_general(
        stacked, columns, (((0,), (0,)), ((), ())), preferred_element_type=F32
    ).astype(jnp.int32)


def fill_onehot(ref, words):
    q = lax.broadcasted_iota(jnp.int32, ref.shape, 0)
    c = lax.broadcasted_iota(jnp.int32, ref.shape, 1)
    hit = jnp.logical_and(
        lax.rem(q, words) == lax.div(c, 32), lax.div(q, words) == lax.div(lax.rem(c, 32), 8)
    )
    ref[...] = jnp.where(hit, 1.0, 0.0).astype(BF)


def kept(weight, spread_bytes):
    c = lax.broadcasted_iota(jnp.int32, (1, weight.shape[1]), 1)
    bit = jnp.left_shift(1, jnp.bitwise_and(c, 7))
    on = jnp.bitwise_and(spread_bytes, bit) != 0
    return jnp.where(on, weight.astype(F32), 0.0).astype(BF)


def mask_pair(idx, gate, gate_mask, up, up_mask):
    rows, units = gate.shape
    words = gate_mask.shape[1]
    half = units // 2
    step = MASK_ROWS

    def body(idx_ref, g_ref, gm_ref, u_ref, um_ref, keep_ref, send_ref, hot_ref):
        @pl.when(pl.program_id(0) == 0)
        def _():
            fill_onehot(hot_ref, words)

        c = idx_ref[1]
        for which, out_ref in ((c, keep_ref), (1 - c, send_ref)):
            cols = pl.ds(pl.multiple_of(which * half, 128), half)
            hot = hot_ref[:, cols]
            out_ref[:, :half] = kept(g_ref[:, cols], spread(gm_ref[...], hot))
            out_ref[:, half:] = kept(u_ref[:, cols], spread(um_ref[...], hot))

    wide = pl.BlockSpec((step, units), lambda i: (i, 0))
    thin = pl.BlockSpec((words, step), lambda i: (0, i))
    return pl.pallas_call(
        body,
        out_shape=[jax.ShapeDtypeStruct((rows, units), BF)] * 2,
        grid=(rows // step,),
        in_specs=[SMEM, wide, thin, wide, thin],
        out_specs=[wide, wide],
        scratch_shapes=[pltpu.VMEM((4 * words, units), BF)],
        compiler_params=params(16),
        cost_estimate=cost(4e9, 16e6),
        name="mask_pair",
    )(idx, gate, gate_mask.T, up, up_mask.T)


def mask_one(weight, mask):
    rows, cols = weight.shape
    words = mask.shape[1]
    step = MASK_ROWS

    def body(w_ref, m_ref, out_ref, hot_ref):
        @pl.when(pl.program_id(0) == 0)
        def _():
            fill_onehot(hot_ref, words)

        out_ref[...] = kept(w_ref[...], spread(m_ref[...], hot_ref[...]))

    wide = pl.BlockSpec((step, cols), lambda i: (i, 0))
    return pl.pallas_call(
        body,
        out_shape=pltpu.VMEM((rows, cols), BF),
        grid=(rows // step,),
        in_specs=[wide, pl.BlockSpec((words, step), lambda i: (0, i))],
        out_specs=wide,
        scratch_shapes=[pltpu.VMEM((4 * words, cols), BF)],
        compiler_params=params(10),
        cost_estimate=cost(2e9, 8e6),
        name="mask_one",
    )(weight, mask.T)


def assemble(idx, axis, pieces):
    deep = pieces[0].ndim == 3
    count = pieces[0].shape[0] if deep else 1
    block, width = pieces[0].shape[-2:]

    def body(idx_ref, *refs):
        out_ref = refs[-1]
        for e in range(4):
            slot = lax.rem(idx_ref[axis] + 4 - e, 4)
            to = pl.ds(pl.multiple_of(slot * block, block), block)
            for d in range(count):
                out_ref[d, to, :] = refs[e][d] if deep else refs[e][...]

    return pl.pallas_call(
        body,
        out_shape=jax.ShapeDtypeStruct((count, 4 * block, width), BF),
        in_specs=[SMEM] + [VMEM] * 4,
        out_specs=VMEM,
        compiler_params=params(10),
        cost_estimate=cost(1e8, 3e6),
        name="assemble",
    )(idx, *pieces)


def product(idx, k, tile, groups, w_own, w_recv, adds=()):
    tokens, feats = groups[0][0].shape[1:]
    part, cols = w_own.shape
    skip, count = sum(SPLIT[:k]), SPLIT[k]
    rows = 2 * count

    def body(idx_ref, a_ref, b_ref, wo_ref, wr_ref, *rest):
        c = idx_ref[1]
        lhs_ref = rest[-1]
        for i, ref in ((0, a_ref), (1, b_ref)):
            for h in range(2):
                to = i * rows + h * count
                take = pl.ds(h * (tokens // 2) + skip, count)
                for j, core in ((0, c), (1, 1 - c)):
                    lhs_ref[to : to + count, j * part : (j + 1) * part] = ref[
                        0, take, pl.ds(pl.multiple_of(core * part, part), part)
                    ]

        def columns(j, carry):
            cut = pl.ds(pl.multiple_of(j * tile, tile), tile)
            acc = jnp.dot(lhs_ref[:, :part], wo_ref[:, cut], preferred_element_type=F32)
            acc += jnp.dot(lhs_ref[:, part:], wr_ref[:, cut], preferred_element_type=F32)
            for i in range(2):
                total = acc[i * rows : (i + 1) * rows]
                if adds:
                    total += rest[i][:, cut].astype(F32)
                rest[len(adds) + i][:, cut] = total.astype(BF)
            return carry

        lax.fori_loop(0, cols // tile, columns, 0)

    def pick(at):
        return pl.BlockSpec((1, tokens, feats), lambda j: (at, 0, 0))

    w_spec = pl.BlockSpec((part, cols), lambda j: (0, 0))
    flat = pl.BlockSpec((rows, cols), lambda j: (0, 0))
    (one, at_one), (two, at_two) = groups
    return pl.pallas_call(
        body,
        out_shape=[jax.ShapeDtypeStruct((rows, cols), BF)] * 2,
        grid=(1,),
        in_specs=[SMEM, pick(at_one), pick(at_two), w_spec, w_spec] + [flat] * len(adds),
        out_specs=[flat, flat],
        scratch_shapes=[pltpu.VMEM((2 * rows, feats), BF)],
        compiler_params=params(22),
        cost_estimate=cost(4 * rows * feats * cols, 1e7),
        name="product",
    )(idx, one, two, w_own, w_recv, *adds)


def hidden_call(own, left, right):
    rows, cols = own[0].shape
    units = cols // 2

    def body(*refs):
        out_ref = refs[-1]
        for h in range(2):
            def both(cut):
                return sum(refs[2 * i + h][:, cut].astype(F32) for i in range(3))

            gate = both(slice(0, units))
            up = both(slice(units, cols))
            out_ref[h] = (gate / (1.0 + jnp.exp(-gate)) * up).astype(BF)

    return pl.pallas_call(
        body,
        out_shape=jax.ShapeDtypeStruct((2, rows, units), BF),
        in_specs=[VMEM] * 6,
        out_specs=VMEM,
        compiler_params=params(10),
        cost_estimate=cost(1e9, 4e6),
        name="hidden",
    )(*own, *left, *right)


def cut_half(array, at):
    _, rows, cols = array.shape

    def body(in_ref, out_ref):
        out_ref[...] = in_ref[0]

    return pl.pallas_call(
        body,
        out_shape=jax.ShapeDtypeStruct((rows, cols), array.dtype),
        grid=(1,),
        in_specs=[pl.BlockSpec((1, rows, cols), lambda j: (at, 0, 0))],
        out_specs=pl.BlockSpec((rows, cols), lambda j: (0, 0)),
        compiler_params=params(2),
        cost_estimate=cost(1e7, 4e5),
        name="cut_half",
    )(array)


def down_call(idx, dists, mine, theirs, weight, to_hbm):
    head = mine[0][0]
    rows, units = (head[0] if isinstance(head, tuple) else head).shape[-2:]
    cols = weight.shape[1]
    quarter = rows // 2
    sources = [pair for both in zip(mine, theirs) for pair in both]
    flat, places = [], []
    for pair in sources:
        for item in pair:
            array, at = item if isinstance(item, tuple) else (item, None)
            if not any(array is f for f in flat):
                flat.append(array)
            places.append((next(i for i, f in enumerate(flat) if f is array), at))
    n_in = len(flat)

    def body(idx_ref, *refs):
        w_ref = refs[n_in]
        out_ref, sq_ref, lhs_ref = refs[-3:]
        x = idx_ref[0]
        c = idx_ref[1]

        def load(n):
            i, at = places[n]
            return refs[i][...] if at is None else refs[i][at]

        halves = (c, 1 - c)

        @pl.when(pl.program_id(0) == 0)
        def _():
            for i, d in enumerate(dists):
                chip = lax.rem(x + 4 - d, 4)
                for u in range(2):
                    for s in range(2):
                        v = load(4 * i + 2 * u + s)
                        at = (2 * i + s) * rows
                        lhs_ref[at : at + rows, u * units : (u + 1) * units] = v
                        v = v.astype(F32)
                        cut = pl.ds(pl.multiple_of(halves[u] * units, 128), units)
                        sq_ref[2 * chip + halves[s], :, cut] = jnp.sum(
                            (v * v).reshape(-1, 8, units), axis=0
                        )

        own_rows = pl.ds(pl.multiple_of(c * units, 128), units)
        other_rows = pl.ds(pl.multiple_of((1 - c) * units, 128), units)
        acc = jnp.dot(lhs_ref[:, :units], w_ref[own_rows, :], preferred_element_type=F32)
        acc += jnp.dot(lhs_ref[:, units:], w_ref[other_rows, :], preferred_element_type=F32)
        out = acc.astype(BF)
        for i, d in enumerate(dists):
            z = lax.rem(x + 4 - d, 4)
            for s in range(2):
                for h in range(2):
                    lo = (2 * i + s) * rows + h * quarter
                    out_ref[4 * z + 2 * halves[s] + h] = out[lo : lo + quarter]

    def whole(a):
        return pl.BlockSpec(a.shape, lambda i, idx_ref: (0,) * a.ndim)

    out_shape = [
        (pltpu.HBM if to_hbm else jax.ShapeDtypeStruct)((16, quarter, cols), BF),
        jax.ShapeDtypeStruct((8, 8, 2 * units), F32),
    ]
    args = [*flat, weight]
    return pl.pallas_call(
        body,
        out_shape=out_shape,
        grid_spec=pltpu.PrefetchScalarGridSpec(
            num_scalar_prefetch=1,
            grid=(cols // DOWN_TILE,),
            in_specs=[whole(a) for a in flat]
            + [pl.BlockSpec((2 * units, DOWN_TILE), lambda i, idx_ref: (0, i))],
            out_specs=[
                pl.BlockSpec((16, quarter, DOWN_TILE), lambda i, idx_ref: (0, 0, i)),
                whole(out_shape[1]),
            ],
            scratch_shapes=[pltpu.VMEM((2 * len(dists) * rows, 2 * units), BF)],
        ),
        compiler_params=params(20),
        cost_estimate=cost(1e9 * len(dists), 8e6),
        name="down",
    )(idx, *args)


def last_block(idx_ref, pairs, w_ref, sq_ref, lhs_ref, block_ref):
    rows, units = pairs[0][0].shape
    quarter = rows // 2
    c = idx_ref[1]
    cores = (c, 1 - c)
    for u, pair in enumerate(pairs):
        cut = pl.ds(pl.multiple_of(cores[u] * units, 128), units)
        for s in range(2):
            v = pair[s][...]
            lhs_ref[s * rows : (s + 1) * rows, u * units : (u + 1) * units] = v
            v = v.astype(F32)
            sq_ref[cores[s], :, cut] = jnp.sum((v * v).reshape(-1, 8, units), axis=0)
    own_rows = pl.ds(pl.multiple_of(c * units, 128), units)
    other_rows = pl.ds(pl.multiple_of((1 - c) * units, 128), units)
    acc = jnp.dot(lhs_ref[:, :units], w_ref[own_rows, :], preferred_element_type=F32)
    acc += jnp.dot(lhs_ref[:, units:], w_ref[other_rows, :], preferred_element_type=F32)
    out = acc.astype(BF)
    for s in range(2):
        for h in range(2):
            lo = s * rows + h * quarter
            block_ref[2 * cores[s] + h] = out[lo : lo + quarter]


def patch_call(idx, mine, theirs, weight, part):
    rows, units = mine[0].shape
    cols = weight.shape[1]

    def body(idx_ref, ma, mb, ta, tb, w_ref, out_in, sq_in, out_ref, sq_ref, lhs_ref):
        del out_in, sq_in
        last_block(idx_ref, ((ma, mb), (ta, tb)), w_ref, sq_ref, lhs_ref, out_ref)

    def whole(a):
        return pl.BlockSpec(a.shape, lambda i, idx_ref: (0,) * a.ndim)

    def place(i, idx_ref):
        return (lax.rem(idx_ref[0] + 2, 4), 0, 0)

    args = [*mine, *theirs, weight]
    return pl.pallas_call(
        body,
        out_shape=[
            pltpu.HBM((16, rows // 2, cols), BF),
            jax.ShapeDtypeStruct((8, 8, 2 * units), F32),
        ],
        grid_spec=pltpu.PrefetchScalarGridSpec(
            num_scalar_prefetch=1,
            grid=(1,),
            in_specs=[whole(a) for a in args] + [pl.BlockSpec(memory_space=pl.ANY)] * 2,
            out_specs=[
                pl.BlockSpec((4, rows // 2, cols), place),
                pl.BlockSpec((2, 8, 2 * units), place),
            ],
            scratch_shapes=[pltpu.VMEM((2 * rows, 2 * units), BF)],
        ),
        input_output_aliases={6: 0, 7: 1},
        compiler_params=params(20),
        cost_estimate=cost(1e9, 8e6),
        name="patch",
    )(idx, *args, in_hbm(part[0]), part[1])


def tail_call(idx, mine, theirs, weight, part):
    rows, units = mine[0].shape
    cols = weight.shape[1]
    quarter = rows // 2
    half = cols // 2

    def body(idx_ref, ma, mb, ta, tb, w_ref, part_ref, sq_in, *refs):
        del sq_in
        by_z, by_y = refs[0:4], refs[4:8]
        sq_ref, lhs_ref, block_ref = refs[8:]
        x, z, y = (idx_ref[i] for i in (0, 2, 3))
        last_block(idx_ref, ((ma, mb), (ta, tb)), w_ref, sq_ref, lhs_ref, block_ref)
        last = lax.rem(x + 2, 4)
        for e in range(4):
            to_z = lax.rem(z + e, 4)

            @pl.when(to_z == last)
            def _():
                by_z[e][...] = block_ref[:, :, :half]

            @pl.when(to_z != last)
            def _():
                by_z[e][...] = part_ref[pl.ds(4 * to_z, 4), :, :half]

            to_y = lax.rem(y + e, 4)
            for i in range(4):
                by_y[e][i] = part_ref[4 * i + to_y, :, half:]
            by_y[e][last] = block_ref[to_y, :, half:]

    def whole(a):
        return pl.BlockSpec(a.shape, lambda i, idx_ref: (0,) * len(a.shape))

    cut = jax.ShapeDtypeStruct((4, quarter, half), BF)
    args = [*mine, *theirs, weight, *part]
    res = pl.pallas_call(
        body,
        out_shape=[cut] * 8 + [jax.ShapeDtypeStruct((8, 8, 2 * units), F32)],
        grid_spec=pltpu.PrefetchScalarGridSpec(
            num_scalar_prefetch=1,
            grid=(1,),
            in_specs=[whole(a) for a in args[:-1]] + [pl.BlockSpec(memory_space=pl.ANY)],
            out_specs=[whole(cut)] * 8
            + [pl.BlockSpec((2, 8, 2 * units), lambda i, r: (lax.rem(r[0] + 2, 4), 0, 0))],
            scratch_shapes=[
                pltpu.VMEM((2 * rows, 2 * units), BF),
                pltpu.VMEM((4, quarter, cols), BF),
            ],
        ),
        input_output_aliases={7: 8},
        compiler_params=params(20),
        cost_estimate=cost(1e9, 8e6),
        name="tail",
    )(idx, *args)
    return res[:4], res[4:8], res[8]


def phase_sum(idx, axis, pieces):
    _, rows, cols = pieces[0].shape

    def body(idx_ref, *refs):
        ins, outs = refs[:4], refs[4:]
        for e in range(4):
            to = lax.rem(idx_ref[axis] + e, 4)
            outs[e][...] = sum(ref[to].astype(F32) for ref in ins).astype(BF)

    return pl.pallas_call(
        body,
        out_shape=[jax.ShapeDtypeStruct((rows, cols), BF)] * 4,
        in_specs=[SMEM] + [VMEM] * 4,
        out_specs=[VMEM] * 4,
        compiler_params=params(6),
        cost_estimate=cost(1e8, 2e6),
        name="phase_sum",
    )(idx, *pieces)


def final_sum(first, left, right):
    rows, cols = left[0].shape
    top = first.shape[0]

    def body(f_ref, *refs):
        out_ref = refs[-1]
        out_ref[:top] = f_ref[...]
        for i in range(2):
            total = sum(ref[...].astype(F32) for ref in refs[4 * i : 4 * i + 4])
            out_ref[top:, i * cols : (i + 1) * cols] = total.astype(BF)

    return pl.pallas_call(
        body,
        out_shape=jax.ShapeDtypeStruct((top + rows, 2 * cols), BF),
        in_specs=[VMEM] * 9,
        out_specs=VMEM,
        compiler_params=params(4),
        cost_estimate=cost(1e8, 2e6),
        name="final_sum",
    )(first, *left, *right)


def column_squares(idx, arrays):
    part = arrays[0].shape[2] // 2

    def body(*refs):
        total = jnp.zeros((8, part), F32)
        for ref in refs[1:-1]:
            for i in range(ref.shape[0]):
                v = ref[i].astype(F32)
                v = (v * v).reshape(-1, 8, part)
                total += jnp.sum(v, axis=0)
        refs[-1][...] = jnp.sum(total, axis=0, keepdims=True)

    def spec(a):
        return pl.BlockSpec((a.shape[0], a.shape[1], part), lambda i, idx_ref: (0, 0, idx_ref[1]))

    return pl.pallas_call(
        lambda *refs: body(*refs),
        out_shape=jax.ShapeDtypeStruct((1, part), F32),
        grid_spec=pltpu.PrefetchScalarGridSpec(
            num_scalar_prefetch=1,
            grid=(1,),
            in_specs=[spec(a) for a in arrays],
            out_specs=pl.BlockSpec((1, part), lambda i, idx_ref: (0, 0)),
        ),
        compiler_params=params(14),
        cost_estimate=cost(1e9, 4e6),
        name="squares",
    )(idx, *arrays)


def summed(parts):
    count, rows, cols = parts.shape
    tile = cols // 4

    def body(p_ref, out_ref):
        total = p_ref[0].astype(F32)
        for i in range(1, count):
            total += p_ref[i].astype(F32)
        out_ref[...] = total.astype(BF)

    return pl.pallas_call(
        body,
        out_shape=jax.ShapeDtypeStruct((rows, cols), BF),
        grid=(4,),
        in_specs=[pl.BlockSpec((count, rows, tile), lambda j: (0, 0, j))],
        out_specs=pl.BlockSpec((rows, tile), lambda j: (0, j)),
        compiler_params=params(8),
        cost_estimate=cost(1e8, 4e6),
        name="summed",
    )(parts)


def step(
    tokens, norm_gain, gate_weight, gate_mask, up_weight, up_mask, down_weight, down_mask
):
    idx = jnp.stack([lax.axis_index(a) for a in ("x", "c", "z", "y")]).astype(jnp.int32)
    (two,) = norm_call(idx, tokens, norm_gain, (2,), 2)
    one, three = norm_call(idx, tokens, norm_gain, (1, 3), 3)
    (own_x,) = norm_call(idx, tokens, norm_gain, (0,))
    own_x = own_x[None]
    got = {d: shift(v, "x", d) for d, v in ((2, two), (1, one), (3, three))}
    own_theirs = swap(own_x)
    w_own, w_send = mask_pair(idx, gate_weight, gate_mask, up_weight, up_mask)
    w_recv = swap(w_send)
    far = [got[2]] + [shift(got[2], "z", e) for e in (1, 2, 3)]
    near = jnp.stack([got[1], got[3]])
    near = [near] + [shift(near, "y", e) for e in (1, 2, 3)]
    far = assemble(idx, 2, far)
    far_theirs = swap(far)
    near = assemble(idx, 3, near)
    near_theirs = swap(near)
    down_kept = mask_one(down_weight, down_mask)

    tiles = (FULL_TILE, SMALL_TILE)
    hid = []
    for k in range(len(SPLIT)):
        w = (w_own, w_recv)
        far_a, far_b = product(idx, k, tiles[k], ((far, 0), (far_theirs, 0)), *w)
        from_left = shift(far_a, "x", 1)
        from_right = shift(far_b, "x", 3)
        groups = ((near_theirs, 1), (near, 0))
        free_b, free_a = product(idx, k, tiles[k], groups, *w)
        left_b = shift(free_b, "x", 1)
        right_a = shift(free_a, "x", 3)
        groups = ((own_x, 0), (own_theirs, 0))
        own = product(idx, k, SMALL_TILE, groups, *w)
        groups = ((near, 1), (near_theirs, 0))
        sums = (from_left, from_right)
        bound_a, bound_b = product(idx, k, tiles[k], groups, *w, sums)
        left_a = shift(bound_a, "x", 1)
        right_b = shift(bound_b, "x", 3)
        hid.append(hidden_call(own, (left_a, left_b), (right_a, right_b)))
    squares = []
    for k in range(len(SPLIT)):
        h0 = hid[k]
        h1 = shift(h0, "x", 1)
        h3 = shift(h0, "x", 3)
        h2a = shift(cut_half(h1, 0), "x", 1)
        h2b = shift(cut_half(h3, 1), "x", 3)
        p0, p1, p3 = swap(h0), swap(h1), swap(h3)
        p2a, p2b = swap(h2a), swap(h2b)
        mine = [((h, 0), (h, 1)) for h in (h0, h1, h3)]
        theirs = [((p, 1), (p, 0)) for p in (p0, p1, p3)]
        at_first = in_vmem(down_kept) if k == 0 else in_hbm(down_kept)
        part = down_call(idx, (0, 1, 3), mine, theirs, at_first, k == 0)
        if k == 0:
            out, sq = patch_call(idx, (h2a, h2b), (p2b, p2a), down_kept, part)
            parts = lax.all_to_all(out, MP, 0, 0, tiled=True).reshape(out.shape)
            mixed = summed(parts)
        else:
            by_z, by_y, sq = tail_call(idx, (h2a, h2b), (p2b, p2a), down_kept, part)
            by_z = [by_z[0]] + [shift(by_z[e], "z", e) for e in (1, 2, 3)]
            by_y = [by_y[0]] + [shift(by_y[e], "y", e) for e in (1, 2, 3)]
            left = phase_sum(idx, 3, by_z)
            left = [left[0]] + [shift(left[e], "y", e) for e in (1, 2, 3)]
            right = phase_sum(idx, 2, by_y)
            right = [right[0]] + [shift(right[e], "z", e) for e in (1, 2, 3)]
            mixed = final_sum(mixed, left, right)
        squares.append(sq)

    sums = column_squares(idx, [own_x, own_theirs, far, far_theirs, near, near_theirs])
    input_norms = jnp.sqrt(sums[0])
    hidden_norms = jnp.sqrt(jnp.sum(squares[0] + squares[1], axis=(0, 1)))
    return (mixed, input_norms, hidden_norms)


def solution(mesh):
    finer = Mesh(mesh.devices.reshape(4, 2, 4, 4), DP + MP)
    in_specs = (
        P(DP, None),
        P(),
        P(DP, MP),
        P(DP, MP),
        P(DP, MP),
        P(DP, MP),
        P(MP, DP),
        P(MP, DP),
    )
    out_specs = (P(MP, DP), P(DP), P(MP))
    return jax.shard_map(step, mesh=finer, in_specs=in_specs, out_specs=out_specs, check_vma=False)
```

time: 347 us -> 249 us (0.72)
  waiting for transfers between devices: 217 us -> 97.3 us
  Pallas kernels: 0 us -> 72.1 us
  starting transfers between devices: 9.37 us -> 69.6 us
  other arithmetic: 40.8 us -> 0.18 us
  matrix products: 32.5 us -> 0 us
  local copies, waits for them, and re-layouts: 32.7 us -> 8.02 us
  between operations: 13.9 us -> 1.16 us
    reduce_scatter x3 -> x0, waiting for transfers between devices: 146 us -> none  [the longest x1 83.1 us: on_device(): lax.psum_scatter(jnp.concatenate([gate_part, up_part], axis=1).astype(jnp...]
    ppermute x0 -> x55, waiting for transfers between devices: none -> 97.3 us  [the longest x41 97.3 us: shift(): lax.ppermute(array, axis, [(i, (i + by) % size) for i in range(size)])]
    pallas_call x0 -> x30, Pallas kernels: none -> 72.1 us  [the longest x8 26.8 us: product(): pl.pallas_call(body, out_shape=[jax.ShapeDtypeStruct((rows, cols), BF)] *...]
    ppermute x0 -> x55, starting transfers between devices: none -> 65.2 us  [the longest x41 62.3 us: shift(): lax.ppermute(array, axis, [(i, (i + by) % size) for i in range(size)])]
    all_gather x1 -> x0, waiting for transfers between devices: 37.9 us -> none  [on_device(): lax.all_gather(hidden, 'dp', axis=0, tiled=True)]
    all_to_all x2 -> x1, waiting for transfers between devices: 32.5 us -> 0.01 us  [step(): parts = lax.all_to_all(out, MP, 0, 0, tiled=True).reshape(out.shape)]
    dot_general x3 -> x0, matrix products: 32.5 us -> none  [the longest x1 13.2 us: on_device(): jnp.dot(lax.all_gather(hidden, 'dp', axis=0, tiled=True), down_kept, pref...]
    unnamed x18 -> x36, local copies, waits for them, and re-layouts: 24.2 us -> 6.81 us
  transfers between devices with their start and end apart: 6 -> 56, of which waited for: 6 -> 16; matrix products, arithmetic and copies ran while one was open for 10% -> 1% of each run, Pallas kernels for 0% -> 26%
where the time goes in v1:
time: 249 us; the launch traced here: 248 us
  waiting for transfers between devices  97.3 us (39%)
  Pallas kernels  72.1 us (29%)
  starting transfers between devices  69.6 us (28%)
  local copies, waits for them, and re-layouts  8.02 us (3%)
    ppermute x41, waiting for transfers between devices, shift(): lax.ppermute(array, axis, [(i, (i + by) % size) for i in range(size)])  97.3 us
    ppermute x41, starting transfers between devices, shift(): lax.ppermute(array, axis, [(i, (i + by) % size) for i in range(size)])  62.3 us
    pallas_call x8, Pallas kernels, product(): pl.pallas_call(body, out_shape=[jax.ShapeDtypeStruct((rows, cols), BF)] *...  26.8 us
    pallas_call x2, Pallas kernels, down_call(): pl.pallas_call(body, out_shape=out_shape, grid_spec=pltpu.PrefetchScalarG...  12.4 us
    pallas_call x3, Pallas kernels, norm_call(): pl.pallas_call(body, out_shape=[jax.ShapeDtypeStruct((steps * block, part...  7.51 us
    unnamed x36, local copies, waits for them, and re-layouts  6.81 us
    pallas_call x1, Pallas kernels, mask_pair(): pl.pallas_call(body, out_shape=[jax.ShapeDtypeStruct((rows, units), BF)]...  5.9 us
  transfers between devices with their start and end apart: 56, of which 16 were waited for; matrix products, arithmetic and copies ran while one was open for 1% of the time, Pallas kernels for 26%

profile of v1, /device:TPU:0, one launch (start us, length us, event | category | flops | bytes accessed | tf_op | source)
XLA Modules:
  0.0 248.4 jit_solution(15515983119977118761)
XLA Ops:
  6.7 5.9 %mask_pair.1 = (bf16[1024,1792]{1,0:T(8,128)(2,1)S(1)}, bf16[1024,1792]{1,0:T(8,128)(2,1)S(1)}) custom-call(s32[4]{0:T(128)S(1)} %pad_add_fusion.idx_ref.refs_0_, bf16[1024,1792]{1,0:T(8,128)(2,1)S(1)} %copy-done.14, s32[56,1024]{1,0:T(8,128)S(1)} %bitcast.17, bf16[1024,1792]{1,0:T(8,128)(2,1)S(1)} %copy-done.15, s32[56,1024]{1,0:T(8,128)S(1)} %bitcast.18), custom_call_target="tpu_custom_call" | custom-call | flops 4000000000 | bytes 16000000 | tf_op jit(solution)/shard_map/mask_pair/pallas_call | solution.py:136
  18.2 6.7 %collective-permute-done.2 = bf16[64,2048]{1,0:T(8,128)(2,1)S(1)} collective-permute-done((bf16[64,2048]{1,0:T(8,128)(2,1)S(1)}, bf16[64,2048]{1,0:T(8,128)(2,1)S(1)}, u32[]{:S(2)}, u32[]{:S(2)}) %collective-permute-start.2) | collective-permute-done | bytes 262176 | tf_op jit(solution)/shard_map/ppermute | solution.py:42
  25.1 3.1 %collective-permute-start.6 = (bf16[2,64,2048]{2,1,0:T(8,128)(2,1)S(1)}, bf16[2,64,2048]{2,1,0:T(8,128)(2,1)S(1)}, u32[]{:S(2)}, u32[]{:S(2)}) collective-permute-start(bf16[2,64,2048]{2,1,0:T(8,128)(2,1)S(1)} %pad_maximum_fusion.refs_0_), channel_id=1, source_target_pairs={{0,3},{1,0},{2,1},{3,2},{4,7},{5,4},{6,5},{7,6},{8,11},{9,8},{10,9... | collective-permute-start | bytes 1572872 | tf_op jit(solution)/shard_map/ppermute | solution.py:42
  29.8 20.6 %collective-permute-done.6.refs_3_ = bf16[2,64,2048]{2,1,0:T(8,128)(2,1)S(1)} collective-permute-done((bf16[2,64,2048]{2,1,0:T(8,128)(2,1)S(1)}, bf16[2,64,2048]{2,1,0:T(8,128)(2,1)S(1)}, u32[]{:S(2)}, u32[]{:S(2)}) %collective-permute-start.6) | collective-permute-done | bytes 524320 | tf_op jit(solution)/shard_map/ppermute | solution.py:42
  50.4 3.7 %collective-permute-done.4.refs_1_ = bf16[2,64,2048]{2,1,0:T(8,128)(2,1)S(1)} collective-permute-done((bf16[2,64,2048]{2,1,0:T(8,128)(2,1)S(1)}, bf16[2,64,2048]{2,1,0:T(8,128)(2,1)S(1)}, u32[]{:S(2)}, u32[]{:S(2)}) %collective-permute-start.4) | collective-permute-done | bytes 524320 | tf_op jit(solution)/shard_map/ppermute | solution.py:42
  59.5 7.8 %collective-permute-done.8.refs_0_ = bf16[64,2048]{1,0:T(8,128)(2,1)S(1)} collective-permute-done((bf16[64,2048]{1,0:T(8,128)(2,1)S(1)}, bf16[64,2048]{1,0:T(8,128)(2,1)S(1)}, u32[]{:S(2)}, u32[]{:S(2)}) %collective-permute-start.8) | collective-permute-done | bytes 262176 | tf_op jit(solution)/shard_map/ppermute | solution.py:42
  67.3 4.0 %collective-permute-start.11 = (bf16[64,2048]{1,0:T(8,128)(2,1)S(1)}, bf16[64,2048]{1,0:T(8,128)(2,1)S(1)}, u32[]{:S(2)}, u32[]{:S(2)}) collective-permute-start(bf16[64,2048]{1,0:T(8,128)(2,1)S(1)} %collective-permute-done.8.refs_0_), channel_id=1, source_target_pairs={{0,12},{4,0},{8,4},{12,8},{1,13},{5,1},{9,5},{13,9},{2,14},{6,2},{... | collective-permute-start | bytes 786440 | tf_op jit(solution)/shard_map/ppermute | solution.py:42
  72.6 9.7 %collective-permute-done.11.refs_3_ = bf16[64,2048]{1,0:T(8,128)(2,1)S(1)} collective-permute-done((bf16[64,2048]{1,0:T(8,128)(2,1)S(1)}, bf16[64,2048]{1,0:T(8,128)(2,1)S(1)}, u32[]{:S(2)}, u32[]{:S(2)}) %collective-permute-start.11) | collective-permute-done | bytes 262176 | tf_op jit(solution)/shard_map/ppermute | solution.py:42
  82.3 3.4 %collective-permute-done.9.refs_1_ = bf16[64,2048]{1,0:T(8,128)(2,1)S(1)} collective-permute-done((bf16[64,2048]{1,0:T(8,128)(2,1)S(1)}, bf16[64,2048]{1,0:T(8,128)(2,1)S(1)}, u32[]{:S(2)}, u32[]{:S(2)}) %collective-permute-start.9) | collective-permute-done | bytes 262176 | tf_op jit(solution)/shard_map/ppermute | solution.py:42
  86.4 3.2 %norm.3 = bf16[256,2048]{1,0:T(8,128)(2,1)S(1)} custom-call(s32[4]{0:T(128)S(1)} %pad_add_fusion.idx_ref.refs_0_, bf16[256,8192]{1,0:T(8,128)(2,1)} %tok_hbm.5, f32[1,8192]{1,0:T(1,128)} %bitcast.23), custom_call_target="tpu_custom_call" | custom-call | flops 2000000000 | bytes 8000000 | tf_op jit(solution)/shard_map/norm/pallas_call | solution.py:76
  98.9 3.2 %collective-permute-start.17 = (bf16[128,1792]{1,0:T(8,128)(2,1)S(1)}, bf16[128,1792]{1,0:T(8,128)(2,1)S(1)}, u32[]{:S(2)}, u32[]{:S(2)}) collective-permute-start(bf16[128,1792]{1,0:T(8,128)(2,1)S(1)} %get-tuple-element.56), channel_id=1, source_target_pairs={{0,96},{32,0},{64,32},{96,64},{1,97},{33,1},{65,33},{97,65},{2,98}... | collective-permute-start | bytes 1376264 | tf_op jit(solution)/shard_map/ppermute | solution.py:42
  102.1 5.4 %collective-permute-done.13.rest_0_ = bf16[128,1792]{1,0:T(8,128)(2,1)S(1)} collective-permute-done((bf16[128,1792]{1,0:T(8,128)(2,1)S(1)}, bf16[128,1792]{1,0:T(8,128)(2,1)S(1)}, u32[]{:S(2)}, u32[]{:S(2)}) %collective-permute-start.13) | collective-permute-done | bytes 458784 | tf_op jit(solution)/shard_map/ppermute | solution.py:42
  113.5 3.8 %product.13 = (bf16[128,1792]{1,0:T(8,128)(2,1)S(1)}, bf16[128,1792]{1,0:T(8,128)(2,1)S(1)}) custom-call(s32[4]{0:T(128)S(1)} %pad_add_fusion.idx_ref.refs_0_, bf16[1,256,2048]{2,1,0:T(8,128)(2,1)S(1)} %assemble.3.a_ref.refs_3_, bf16[1,256,2048]{2,1,0:T(8,128)(2,1)S(1)} %collective-permute-done.12.b_ref.refs_4_, ...), custom_call_target="tpu_custom_call" | custom-call | flops 1879048192 | bytes 10000000 | tf_op jit(solution)/shard_map/product/pallas_call | solution.py:236
  117.4 3.2 %collective-permute-start.29 = (bf16[128,1792]{1,0:T(8,128)(2,1)S(1)}, bf16[128,1792]{1,0:T(8,128)(2,1)S(1)}, u32[]{:S(2)}, u32[]{:S(2)}) collective-permute-start(bf16[128,1792]{1,0:T(8,128)(2,1)S(1)} %get-tuple-element.64), channel_id=1, source_target_pairs={{0,96},{32,0},{64,32},{96,64},{1,97},{33,1},{65,33},{97,65},{2,98}... | collective-permute-start | bytes 1376264 | tf_op jit(solution)/shard_map/ppermute | solution.py:42
  120.6 3.8 %product.15 = (bf16[128,1792]{1,0:T(8,128)(2,1)S(1)}, bf16[128,1792]{1,0:T(8,128)(2,1)S(1)}) custom-call(s32[4]{0:T(128)S(1)} %pad_add_fusion.idx_ref.refs_0_, bf16[2,256,2048]{2,1,0:T(8,128)(2,1)S(1)} %collective-permute-done.7.b_ref.a_ref.refs_6_, bf16[2,256,2048]{2,1,0:T(8,128)(2,1)S(1)} %assemble.2.a_ref.b_ref.refs_5_, ...), custom_call_target="tpu_custom_call" | custom-call | flops 1879048192 | bytes 10000000 | tf_op jit(solution)/shard_map/product/pallas_call | solution.py:236
  124.5 3.8 %product.8 = (bf16[128,1792]{1,0:T(8,128)(2,1)S(1)}, bf16[128,1792]{1,0:T(8,128)(2,1)S(1)}) custom-call(s32[4]{0:T(128)S(1)} %pad_add_fusion.idx_ref.refs_0_, bf16[1,256,2048]{2,1,0:T(8,128)(2,1)S(1)} %bitcast.13, bf16[1,256,2048]{2,1,0:T(8,128)(2,1)S(1)} %collective-permute-done.b_ref.refs_2_, bf16[1024,1792]{1,0:T(8,128)(2,1)S(1)} %get-tuple-element.46.wo_ref, ...), custom_call_target="tpu_custom_call" | custom-call | flops 1879048192 | bytes 10000000 | tf_op jit(solution)/shard_map/product/pallas_call | solution.py:236
  128.3 3.3 %collective-permute-start.32 = (bf16[128,1792]{1,0:T(8,128)(2,1)S(1)}, bf16[128,1792]{1,0:T(8,128)(2,1)S(1)}, u32[]{:S(2)}, u32[]{:S(2)}) collective-permute-start(bf16[128,1792]{1,0:T(8,128)(2,1)S(1)} %get-tuple-element.67), channel_id=1, source_target_pairs={{0,96},{32,0},{64,32},{96,64},{1,97},{33,1},{65,33},{97,65},{2,98}... | collective-permute-start | bytes 1376264 | tf_op jit(solution)/shard_map/ppermute | solution.py:42
  132.3 4.7 %collective-permute-done.28.rest_0_ = bf16[128,1792]{1,0:T(8,128)(2,1)S(1)} collective-permute-done((bf16[128,1792]{1,0:T(8,128)(2,1)S(1)}, bf16[128,1792]{1,0:T(8,128)(2,1)S(1)}, u32[]{:S(2)}, u32[]{:S(2)}) %collective-permute-start.28) | collective-permute-done | bytes 458784 | tf_op jit(solution)/shard_map/ppermute | solution.py:42
  137.0 3.8 %product.14 = (bf16[128,1792]{1,0:T(8,128)(2,1)S(1)}, bf16[128,1792]{1,0:T(8,128)(2,1)S(1)}) custom-call(s32[4]{0:T(128)S(1)} %pad_add_fusion.idx_ref.refs_0_, bf16[2,256,2048]{2,1,0:T(8,128)(2,1)S(1)} %assemble.2.a_ref.b_ref.refs_5_, bf16[2,256,2048]{2,1,0:T(8,128)(2,1)S(1)} %collective-permute-done.7.b_ref.a_ref.refs_6_, ...), custom_call_target="tpu_custom_call" | custom-call | flops 1879048192 | bytes 10000000 | tf_op jit(solution)/shard_map/product/pallas_call | solution.py:236
  142.1 4.7 %collective-permute-done.31.refs_3_ = bf16[128,1792]{1,0:T(8,128)(2,1)S(1)} collective-permute-done((bf16[128,1792]{1,0:T(8,128)(2,1)S(1)}, bf16[128,1792]{1,0:T(8,128)(2,1)S(1)}, u32[]{:S(2)}, u32[]{:S(2)}) %collective-permute-start.31) | collective-permute-done | bytes 458784 | tf_op jit(solution)/shard_map/ppermute | solution.py:42
  148.3 8.4 %collective-permute-done.21.in_ref.refs_4_ = bf16[2,128,896]{2,1,0:T(8,128)(2,1)S(1)} collective-permute-done((bf16[2,128,896]{2,1,0:T(8,128)(2,1)S(1)}, bf16[2,128,896]{2,1,0:T(8,128)(2,1)S(1)}, u32[]{:S(2)}, u32[]{:S(2)}) %collective-permute-start.21) | collective-permute-done | bytes 458784 | tf_op jit(solution)/shard_map/ppermute | solution.py:42
  157.2 4.4 %mask_one.1.refs_6_.w_ref = bf16[1792,1024]{1,0:T(8,128)(2,1)S(1)} custom-call(bf16[1792,1024]{1,0:T(8,128)(2,1)S(1)} %copy-done.10, s32[32,1792]{1,0:T(8,128)S(1)} %bitcast.16), custom_call_target="tpu_custom_call" | custom-call | flops 2000000000 | bytes 8000000 | tf_op jit(solution)/shard_map/mask_one/pallas_call | solution.py:162
  161.7 3.8 %collective-permute-done.30.refs_2_ = bf16[128,1792]{1,0:T(8,128)(2,1)S(1)} collective-permute-done((bf16[128,1792]{1,0:T(8,128)(2,1)S(1)}, bf16[128,1792]{1,0:T(8,128)(2,1)S(1)}, u32[]{:S(2)}, u32[]{:S(2)}) %collective-permute-start.30) | collective-permute-done | bytes 458784 | tf_op jit(solution)/shard_map/ppermute | solution.py:42
  167.6 3.8 %product.12 = (bf16[128,1792]{1,0:T(8,128)(2,1)S(1)}, bf16[128,1792]{1,0:T(8,128)(2,1)S(1)}) custom-call(s32[4]{0:T(128)S(1)} %pad_add_fusion.idx_ref.refs_0_, bf16[1,256,2048]{2,1,0:T(8,128)(2,1)S(1)} %bitcast.14, bf16[1,256,2048]{2,1,0:T(8,128)(2,1)S(1)} %collective-permute-done.b_ref.refs_2_, bf16[1024,1792]{1,0:T(8,128)(2,1)S(1)} %get-tuple-element.46.wo_ref, ...), custom_call_target="tpu_custom_call" | custom-call | flops 1879048192 | bytes 10000000 | tf_op jit(solution)/shard_map/product/pallas_call | solution.py:236
  176.0 5.8 %down.2 = (bf16[16,64,1024]{2,1,0:T(8,128)(2,1)}, f32[8,8,1792]{2,1,0:T(8,128)S(1)}) custom-call(s32[4]{0:T(128)S(1)} %pad_add_fusion.idx_ref.refs_0_, bf16[2,128,896]{2,1,0:T(8,128)(2,1)S(1)} %hidden.2.refs_0_, bf16[2,128,896]{2,1,0:T(8,128)(2,1)S(1)} %collective-permute-done.25.refs_1_, bf16[2,128,896]{2,1,0:T(8,128)(2,1)S(1)} %collective-permute-done.19.in_ref.refs_2_, ...), custom_call_target="tpu_custom_call" | custom-call | flops 3000000000 | bytes 8000000 | tf_op jit(solution)/shard_map/down/pallas_call | solution.py:354
  185.3 4.4 %all-to-all-start = ((bf16[16,64,1024]{2,1,0:T(8,128)(2,1)}), bf16[16,64,1024]{2,1,0:T(8,128)(2,1)}, u32[]{:S(2)}, u32[]{:S(2)}) async-start(bf16[16,64,1024]{2,1,0:T(8,128)(2,1)} %get-tuple-element.60), calls=%async_computation | async-start | bytes 4194304 | tf_op jit(solution)/shard_map/all_to_all | solution.py:640
  191.6 3.2 %collective-permute-start.37 = (bf16[128,896]{1,0:T(8,128)(2,1)S(1)}, bf16[128,896]{1,0:T(8,128)(2,1)S(1)}, u32[]{:S(2)}, u32[]{:S(2)}) collective-permute-start(bf16[128,896]{1,0:T(8,128)(2,1)S(1)} %cut_half.7), channel_id=1, source_target_pairs={{0,96},{32,0},{64,32},{96,64},{1,97},{33,1},{65,33},{97,65},{2,98}... | collective-permute-start | bytes 688136 | tf_op jit(solution)/shard_map/ppermute | solution.py:42
  195.8 4.2 %collective-permute-done.37.mb = bf16[128,896]{1,0:T(8,128)(2,1)S(1)} collective-permute-done((bf16[128,896]{1,0:T(8,128)(2,1)S(1)}, bf16[128,896]{1,0:T(8,128)(2,1)S(1)}, u32[]{:S(2)}, u32[]{:S(2)}) %collective-permute-start.37) | collective-permute-done | bytes 229408 | tf_op jit(solution)/shard_map/ppermute | solution.py:42
  200.0 4.4 %collective-permute-done.35.ma = bf16[128,896]{1,0:T(8,128)(2,1)S(1)} collective-permute-done((bf16[128,896]{1,0:T(8,128)(2,1)S(1)}, bf16[128,896]{1,0:T(8,128)(2,1)S(1)}, u32[]{:S(2)}, u32[]{:S(2)}) %collective-permute-start.35) | collective-permute-done | bytes 229408 | tf_op jit(solution)/shard_map/ppermute | solution.py:42
  204.5 6.6 %down.3 = (bf16[16,64,1024]{2,1,0:T(8,128)(2,1)S(1)}, f32[8,8,1792]{2,1,0:T(8,128)S(1)}) custom-call(s32[4]{0:T(128)S(1)} %pad_add_fusion.idx_ref.refs_0_, bf16[2,128,896]{2,1,0:T(8,128)(2,1)} %hidden.3.refs_0_, bf16[2,128,896]{2,1,0:T(8,128)(2,1)S(1)} %collective-permute-done.40.refs_1_, bf16[2,128,896]{2,1,0:T(8,128)(2,1)} %collective-permute-done.34.in_ref.refs_2_, ...), custom_call_target="tpu_custom_call" | custom-call | flops 3000000000 | bytes 8000000 | tf_op jit(solution)/shard_map/down/pallas_call | solution.py:354
  214.9 2.7 %collective-permute-start.44 = (bf16[4,64,512]{2,1,0:T(8,128)(2,1)S(1)}, bf16[4,64,512]{2,1,0:T(8,128)(2,1)S(1)}, u32[]{:S(2)}, u32[]{:S(2)}) collective-permute-start(bf16[4,64,512]{2,1,0:T(8,128)(2,1)S(1)} %get-tuple-element.73), channel_id=1, source_target_pairs={{0,8},{4,12},{8,0},{12,4},{1,9},{5,13},{9,1},{13,5},{2,10},{6,14},... | collective-permute-start | bytes 786440 | tf_op jit(solution)/shard_map/ppermute | solution.py:42
  226.0 6.7 %collective-permute-done.44.refs_2_ = bf16[4,64,512]{2,1,0:T(8,128)(2,1)S(1)} collective-permute-done((bf16[4,64,512]{2,1,0:T(8,128)(2,1)S(1)}, bf16[4,64,512]{2,1,0:T(8,128)(2,1)S(1)}, u32[]{:S(2)}, u32[]{:S(2)}) %collective-permute-start.44) | collective-permute-done | bytes 262176 | tf_op jit(solution)/shard_map/ppermute | solution.py:42
  (151 shorter events, 81.0 us)
Async XLA Ops:
  12.6 77.6 %collective-permute-start.1 = (bf16[1024,1792]{1,0:T(8,128)(2,1)S(1)}, bf16[1024,1792]{1,0:T(8,128)(2,1)S(1)}, u32[]{:S(2)}, u32[]{:S(2)}) collective-permute-start(bf16[1024,1792]{1,0:T(8,128)(2,1)S(1)} %get-tuple-element.47), channel_id=1, source_target_pairs={{0,16},{16,0},{1,17},{17,1},{2,18},{18,2},{3,19},{19,3},{4,20},{20... | collective-permute-start | bytes 11010056 | tf_op jit(solution)/shard_map/ppermute | solution.py:46
  25.1 25.3 %collective-permute-start.6 = (bf16[2,64,2048]{2,1,0:T(8,128)(2,1)S(1)}, bf16[2,64,2048]{2,1,0:T(8,128)(2,1)S(1)}, u32[]{:S(2)}, u32[]{:S(2)}) collective-permute-start(bf16[2,64,2048]{2,1,0:T(8,128)(2,1)S(1)} %pad_maximum_fusion.refs_0_), channel_id=1, source_target_pairs={{0,3},{1,0},{2,1},{3,2},{4,7},{5,4},{6,5},{7,6},{8,11},{9,8},{10,9... | collective-permute-start | bytes 1572872 | tf_op jit(solution)/shard_map/ppermute | solution.py:42
  28.2 22.2 %collective-permute-start.5 = (bf16[2,64,2048]{2,1,0:T(8,128)(2,1)S(1)}, bf16[2,64,2048]{2,1,0:T(8,128)(2,1)S(1)}, u32[]{:S(2)}, u32[]{:S(2)}) collective-permute-start(bf16[2,64,2048]{2,1,0:T(8,128)(2,1)S(1)} %pad_maximum_fusion.refs_0_), channel_id=1, source_target_pairs={{0,2},{1,3},{2,0},{3,1},{4,6},{5,7},{6,4},{7,5},{8,10},{9,11},{10,... | collective-permute-start | bytes 1572872 | tf_op jit(solution)/shard_map/ppermute | solution.py:42
  28.8 25.3 %collective-permute-start.4 = (bf16[2,64,2048]{2,1,0:T(8,128)(2,1)S(1)}, bf16[2,64,2048]{2,1,0:T(8,128)(2,1)S(1)}, u32[]{:S(2)}, u32[]{:S(2)}) collective-permute-start(bf16[2,64,2048]{2,1,0:T(8,128)(2,1)S(1)} %pad_maximum_fusion.refs_0_), channel_id=1, source_target_pairs={{0,1},{1,2},{2,3},{3,0},{4,5},{5,6},{6,7},{7,4},{8,9},{9,10},{10,1... | collective-permute-start | bytes 1572872 | tf_op jit(solution)/shard_map/ppermute | solution.py:42
  54.8 41.4 %collective-permute-start.7 = (bf16[2,256,2048]{2,1,0:T(8,128)(2,1)S(1)}, bf16[2,256,2048]{2,1,0:T(8,128)(2,1)S(1)}, u32[]{:S(2)}, u32[]{:S(2)}) collective-permute-start(bf16[2,256,2048]{2,1,0:T(8,128)(2,1)S(1)} %assemble.2.a_ref.b_ref.refs_5_), channel_id=1, source_target_pairs={{0,16},{16,0},{1,17},{17,1},{2,18},{18,2},{3,19},{19,3},{4,20},{20... | collective-permute-start | bytes 6291464 | tf_op jit(solution)/shard_map/ppermute | solution.py:46
  67.3 15.0 %collective-permute-start.11 = (bf16[64,2048]{1,0:T(8,128)(2,1)S(1)}, bf16[64,2048]{1,0:T(8,128)(2,1)S(1)}, u32[]{:S(2)}, u32[]{:S(2)}) collective-permute-start(bf16[64,2048]{1,0:T(8,128)(2,1)S(1)} %collective-permute-done.8.refs_0_), channel_id=1, source_target_pairs={{0,12},{4,0},{8,4},{12,8},{1,13},{5,1},{9,5},{13,9},{2,14},{6,2},{... | collective-permute-start | bytes 786440 | tf_op jit(solution)/shard_map/ppermute | solution.py:42
  71.3 14.4 %collective-permute-start.9 = (bf16[64,2048]{1,0:T(8,128)(2,1)S(1)}, bf16[64,2048]{1,0:T(8,128)(2,1)S(1)}, u32[]{:S(2)}, u32[]{:S(2)}) collective-permute-start(bf16[64,2048]{1,0:T(8,128)(2,1)S(1)} %collective-permute-done.8.refs_0_), channel_id=1, source_target_pairs={{0,4},{4,8},{8,12},{12,0},{1,5},{5,9},{9,13},{13,1},{2,6},{6,10},{... | collective-permute-start | bytes 786440 | tf_op jit(solution)/shard_map/ppermute | solution.py:42
  89.6 27.7 %collective-permute-start = (bf16[1,256,2048]{2,1,0:T(8,128)(2,1)S(1)}, bf16[1,256,2048]{2,1,0:T(8,128)(2,1)S(1)}, u32[]{:S(2)}, u32[]{:S(2)}) collective-permute-start(bf16[1,256,2048]{2,1,0:T(8,128)(2,1)S(1)} %bitcast.12), channel_id=1, source_target_pairs={{0,16},{16,0},{1,17},{17,1},{2,18},{18,2},{3,19},{19,3},{4,20},{20... | collective-permute-start | bytes 3145736 | tf_op jit(solution)/shard_map/ppermute | solution.py:46
  92.8 14.7 %collective-permute-start.13 = (bf16[128,1792]{1,0:T(8,128)(2,1)S(1)}, bf16[128,1792]{1,0:T(8,128)(2,1)S(1)}, u32[]{:S(2)}, u32[]{:S(2)}) collective-permute-start(bf16[128,1792]{1,0:T(8,128)(2,1)S(1)} %get-tuple-element.52), channel_id=1, source_target_pairs={{0,32},{32,64},{64,96},{96,0},{1,33},{33,65},{65,97},{97,1},{2,34}... | collective-permute-start | bytes 1376264 | tf_op jit(solution)/shard_map/ppermute | solution.py:42
  98.8 18.6 %collective-permute-start.16 = (bf16[128,1792]{1,0:T(8,128)(2,1)S(1)}, bf16[128,1792]{1,0:T(8,128)(2,1)S(1)}, u32[]{:S(2)}, u32[]{:S(2)}) collective-permute-start(bf16[128,1792]{1,0:T(8,128)(2,1)S(1)} %get-tuple-element.55), channel_id=1, source_target_pairs={{0,32},{32,64},{64,96},{96,0},{1,33},{33,65},{65,97},{97,1},{2,34}... | collective-permute-start | bytes 1376264 | tf_op jit(solution)/shard_map/ppermute | solution.py:42
  98.9 25.6 %collective-permute-start.17 = (bf16[128,1792]{1,0:T(8,128)(2,1)S(1)}, bf16[128,1792]{1,0:T(8,128)(2,1)S(1)}, u32[]{:S(2)}, u32[]{:S(2)}) collective-permute-start(bf16[128,1792]{1,0:T(8,128)(2,1)S(1)} %get-tuple-element.56), channel_id=1, source_target_pairs={{0,96},{32,0},{64,32},{96,64},{1,97},{33,1},{65,33},{97,65},{2,98}... | collective-permute-start | bytes 1376264 | tf_op jit(solution)/shard_map/ppermute | solution.py:42
  110.2 18.2 %collective-permute-start.15 = (bf16[128,1792]{1,0:T(8,128)(2,1)S(1)}, bf16[128,1792]{1,0:T(8,128)(2,1)S(1)}, u32[]{:S(2)}, u32[]{:S(2)}) collective-permute-start(bf16[128,1792]{1,0:T(8,128)(2,1)S(1)} %get-tuple-element.54), channel_id=1, source_target_pairs={{0,32},{32,64},{64,96},{96,0},{1,33},{33,65},{65,97},{97,1},{2,34}... | collective-permute-start | bytes 1376264 | tf_op jit(solution)/shard_map/ppermute | solution.py:42
  111.4 20.2 %collective-permute-start.18 = (bf16[128,1792]{1,0:T(8,128)(2,1)S(1)}, bf16[128,1792]{1,0:T(8,128)(2,1)S(1)}, u32[]{:S(2)}, u32[]{:S(2)}) collective-permute-start(bf16[128,1792]{1,0:T(8,128)(2,1)S(1)} %get-tuple-element.57), channel_id=1, source_target_pairs={{0,96},{32,0},{64,32},{96,64},{1,97},{33,1},{65,33},{97,65},{2,98}... | collective-permute-start | bytes 1376264 | tf_op jit(solution)/shard_map/ppermute | solution.py:42
  117.3 19.7 %collective-permute-start.28 = (bf16[128,1792]{1,0:T(8,128)(2,1)S(1)}, bf16[128,1792]{1,0:T(8,128)(2,1)S(1)}, u32[]{:S(2)}, u32[]{:S(2)}) collective-permute-start(bf16[128,1792]{1,0:T(8,128)(2,1)S(1)} %get-tuple-element.63), channel_id=1, source_target_pairs={{0,32},{32,64},{64,96},{96,0},{1,33},{33,65},{65,97},{97,1},{2,34}... | collective-permute-start | bytes 1376264 | tf_op jit(solution)/shard_map/ppermute | solution.py:42
  117.4 19.6 %collective-permute-start.29 = (bf16[128,1792]{1,0:T(8,128)(2,1)S(1)}, bf16[128,1792]{1,0:T(8,128)(2,1)S(1)}, u32[]{:S(2)}, u32[]{:S(2)}) collective-permute-start(bf16[128,1792]{1,0:T(8,128)(2,1)S(1)} %get-tuple-element.64), channel_id=1, source_target_pairs={{0,96},{32,0},{64,32},{96,64},{1,97},{33,1},{65,33},{97,65},{2,98}... | collective-permute-start | bytes 1376264 | tf_op jit(solution)/shard_map/ppermute | solution.py:42
  124.4 22.4 %collective-permute-start.31 = (bf16[128,1792]{1,0:T(8,128)(2,1)S(1)}, bf16[128,1792]{1,0:T(8,128)(2,1)S(1)}, u32[]{:S(2)}, u32[]{:S(2)}) collective-permute-start(bf16[128,1792]{1,0:T(8,128)(2,1)S(1)} %get-tuple-element.66), channel_id=1, source_target_pairs={{0,32},{32,64},{64,96},{96,0},{1,33},{33,65},{65,97},{97,1},{2,34}... | collective-permute-start | bytes 1376264 | tf_op jit(solution)/shard_map/ppermute | solution.py:42
  128.3 20.0 %collective-permute-start.32 = (bf16[128,1792]{1,0:T(8,128)(2,1)S(1)}, bf16[128,1792]{1,0:T(8,128)(2,1)S(1)}, u32[]{:S(2)}, u32[]{:S(2)}) collective-permute-start(bf16[128,1792]{1,0:T(8,128)(2,1)S(1)} %get-tuple-element.67), channel_id=1, source_target_pairs={{0,96},{32,0},{64,32},{96,64},{1,97},{33,1},{65,33},{97,65},{2,98}... | collective-permute-start | bytes 1376264 | tf_op jit(solution)/shard_map/ppermute | solution.py:42
  132.2 24.5 %collective-permute-start.21 = (bf16[2,128,896]{2,1,0:T(8,128)(2,1)S(1)}, bf16[2,128,896]{2,1,0:T(8,128)(2,1)S(1)}, u32[]{:S(2)}, u32[]{:S(2)}) collective-permute-start(bf16[2,128,896]{2,1,0:T(8,128)(2,1)S(1)} %hidden.2.refs_0_), channel_id=1, source_target_pairs={{0,96},{32,0},{64,32},{96,64},{1,97},{33,1},{65,33},{97,65},{2,98}... | collective-permute-start | bytes 1376264 | tf_op jit(solution)/shard_map/ppermute | solution.py:42
  137.0 19.7 %collective-permute-start.19 = (bf16[2,128,896]{2,1,0:T(8,128)(2,1)S(1)}, bf16[2,128,896]{2,1,0:T(8,128)(2,1)S(1)}, u32[]{:S(2)}, u32[]{:S(2)}) collective-permute-start(bf16[2,128,896]{2,1,0:T(8,128)(2,1)S(1)} %hidden.2.refs_0_), channel_id=1, source_target_pairs={{0,32},{32,64},{64,96},{96,0},{1,33},{33,65},{65,97},{97,1},{2,34}... | collective-permute-start | bytes 1376264 | tf_op jit(solution)/shard_map/ppermute | solution.py:42
  140.8 24.7 %collective-permute-start.30 = (bf16[128,1792]{1,0:T(8,128)(2,1)S(1)}, bf16[128,1792]{1,0:T(8,128)(2,1)S(1)}, u32[]{:S(2)}, u32[]{:S(2)}) collective-permute-start(bf16[128,1792]{1,0:T(8,128)(2,1)S(1)} %get-tuple-element.65), channel_id=1, source_target_pairs={{0,32},{32,64},{64,96},{96,0},{1,33},{33,65},{65,97},{97,1},{2,34}... | collective-permute-start | bytes 1376264 | tf_op jit(solution)/shard_map/ppermute | solution.py:42
  146.8 20.2 %collective-permute-start.33 = (bf16[128,1792]{1,0:T(8,128)(2,1)S(1)}, bf16[128,1792]{1,0:T(8,128)(2,1)S(1)}, u32[]{:S(2)}, u32[]{:S(2)}) collective-permute-start(bf16[128,1792]{1,0:T(8,128)(2,1)S(1)} %get-tuple-element.68), channel_id=1, source_target_pairs={{0,96},{32,0},{64,32},{96,64},{1,97},{33,1},{65,33},{97,65},{2,98}... | collective-permute-start | bytes 1376264 | tf_op jit(solution)/shard_map/ppermute | solution.py:42
  148.3 24.4 %collective-permute-start.25 = (bf16[2,128,896]{2,1,0:T(8,128)(2,1)S(1)}, bf16[2,128,896]{2,1,0:T(8,128)(2,1)S(1)}, u32[]{:S(2)}, u32[]{:S(2)}) collective-permute-start(bf16[2,128,896]{2,1,0:T(8,128)(2,1)S(1)} %hidden.2.refs_0_), channel_id=1, source_target_pairs={{0,16},{16,0},{1,17},{17,1},{2,18},{18,2},{3,19},{19,3},{4,20},{20... | collective-permute-start | bytes 1376264 | tf_op jit(solution)/shard_map/ppermute | solution.py:46
  156.7 18.8 %collective-permute-start.27 = (bf16[2,128,896]{2,1,0:T(8,128)(2,1)S(1)}, bf16[2,128,896]{2,1,0:T(8,128)(2,1)S(1)}, u32[]{:S(2)}, u32[]{:S(2)}) collective-permute-start(bf16[2,128,896]{2,1,0:T(8,128)(2,1)S(1)} %collective-permute-done.21.in_ref.refs_4_), channel_id=1, source_target_pairs={{0,16},{16,0},{1,17},{17,1},{2,18},{18,2},{3,19},{19,3},{4,20},{20... | collective-permute-start | bytes 1376264 | tf_op jit(solution)/shard_map/ppermute | solution.py:46
  156.7 19.3 %collective-permute-start.26 = (bf16[2,128,896]{2,1,0:T(8,128)(2,1)S(1)}, bf16[2,128,896]{2,1,0:T(8,128)(2,1)S(1)}, u32[]{:S(2)}, u32[]{:S(2)}) collective-permute-start(bf16[2,128,896]{2,1,0:T(8,128)(2,1)S(1)} %collective-permute-done.19.in_ref.refs_2_), channel_id=1, source_target_pairs={{0,16},{16,0},{1,17},{17,1},{2,18},{18,2},{3,19},{19,3},{4,20},{20... | collective-permute-start | bytes 1376264 | tf_op jit(solution)/shard_map/ppermute | solution.py:46
  172.7 17.4 %collective-permute-start.36 = (bf16[2,128,896]{2,1,0:T(8,128)(2,1)}, bf16[2,128,896]{2,1,0:T(8,128)(2,1)}, u32[]{:S(2)}, u32[]{:S(2)}) collective-permute-start(bf16[2,128,896]{2,1,0:T(8,128)(2,1)} %hidden.3.refs_0_), channel_id=1, source_target_pairs={{0,96},{32,0},{64,32},{96,64},{1,97},{33,1},{65,33},{97,65},{2,98}... | collective-permute-start | bytes 1376264 | tf_op jit(solution)/shard_map/ppermute | solution.py:42
  175.4 14.9 %collective-permute-start.34 = (bf16[2,128,896]{2,1,0:T(8,128)(2,1)}, bf16[2,128,896]{2,1,0:T(8,128)(2,1)}, u32[]{:S(2)}, u32[]{:S(2)}) collective-permute-start(bf16[2,128,896]{2,1,0:T(8,128)(2,1)} %hidden.3.refs_0_), channel_id=1, source_target_pairs={{0,32},{32,64},{64,96},{96,0},{1,33},{33,65},{65,97},{97,1},{2,34}... | collective-permute-start | bytes 1376264 | tf_op jit(solution)/shard_map/ppermute | solution.py:42
  185.3 59.9 %all-to-all-start = ((bf16[16,64,1024]{2,1,0:T(8,128)(2,1)}), bf16[16,64,1024]{2,1,0:T(8,128)(2,1)}, u32[]{:S(2)}, u32[]{:S(2)}) async-start(bf16[16,64,1024]{2,1,0:T(8,128)(2,1)} %get-tuple-element.60), calls=%async_computation | async-start | bytes 4194304 | tf_op jit(solution)/shard_map/all_to_all | solution.py:640
  189.7 14.8 %collective-permute-start.40 = (bf16[2,128,896]{2,1,0:T(8,128)(2,1)}, bf16[2,128,896]{2,1,0:T(8,128)(2,1)S(1)}, u32[]{:S(2)}, u32[]{:S(2)}) collective-permute-start(bf16[2,128,896]{2,1,0:T(8,128)(2,1)} %hidden.3.refs_0_), channel_id=1, source_target_pairs={{0,16},{16,0},{1,17},{17,1},{2,18},{18,2},{3,19},{19,3},{4,20},{20... | collective-permute-start | bytes 1376264 | tf_op jit(solution)/shard_map/ppermute | solution.py:46
  214.9 17.8 %collective-permute-start.44 = (bf16[4,64,512]{2,1,0:T(8,128)(2,1)S(1)}, bf16[4,64,512]{2,1,0:T(8,128)(2,1)S(1)}, u32[]{:S(2)}, u32[]{:S(2)}) collective-permute-start(bf16[4,64,512]{2,1,0:T(8,128)(2,1)S(1)} %get-tuple-element.73), channel_id=1, source_target_pairs={{0,8},{4,12},{8,0},{12,4},{1,9},{5,13},{9,1},{13,5},{2,10},{6,14},... | collective-permute-start | bytes 786440 | tf_op jit(solution)/shard_map/ppermute | solution.py:42
  217.6 15.1 %collective-permute-start.45 = (bf16[4,64,512]{2,1,0:T(8,128)(2,1)S(1)}, bf16[4,64,512]{2,1,0:T(8,128)(2,1)S(1)}, u32[]{:S(2)}, u32[]{:S(2)}) collective-permute-start(bf16[4,64,512]{2,1,0:T(8,128)(2,1)S(1)} %get-tuple-element.74), channel_id=1, source_target_pairs={{0,12},{4,0},{8,4},{12,8},{1,13},{5,1},{9,5},{13,9},{2,14},{6,2},{... | collective-permute-start | bytes 786440 | tf_op jit(solution)/shard_map/ppermute | solution.py:42
  219.1 17.2 %collective-permute-start.49 = (bf16[4,64,512]{2,1,0:T(8,128)(2,1)S(1)}, bf16[4,64,512]{2,1,0:T(8,128)(2,1)S(1)}, u32[]{:S(2)}, u32[]{:S(2)}) collective-permute-start(bf16[4,64,512]{2,1,0:T(8,128)(2,1)S(1)} %get-tuple-element.80), channel_id=1, source_target_pairs={{0,1},{1,2},{2,3},{3,0},{4,5},{5,6},{6,7},{7,4},{8,9},{9,10},{10,1... | collective-permute-start | bytes 786440 | tf_op jit(solution)/shard_map/ppermute | solution.py:42
  220.5 18.4 %collective-permute-start.50 = (bf16[4,64,512]{2,1,0:T(8,128)(2,1)S(1)}, bf16[4,64,512]{2,1,0:T(8,128)(2,1)S(1)}, u32[]{:S(2)}, u32[]{:S(2)}) collective-permute-start(bf16[4,64,512]{2,1,0:T(8,128)(2,1)S(1)} %get-tuple-element.81), channel_id=1, source_target_pairs={{0,2},{1,3},{2,0},{3,1},{4,6},{5,7},{6,4},{7,5},{8,10},{9,11},{10,... | collective-permute-start | bytes 786440 | tf_op jit(solution)/shard_map/ppermute | solution.py:42
  (42 other events, 619.9 us)
